TPU v7x, 32 devices: a whole 2x2x4 slice. The times are simulated.
32 devices in a mesh: blk: 8 (over z, x), dp: 4 (over y, core).
Axes of the slice: x: 2, y: 2, z: 4, core: 2. Of those that a mesh axis runs over, the one named last changes fastest.
Arguments:
- embeddings: bfloat16 [8192, 512], P(('dp', 'blk')), may hold values from -16 to 16
- centers: bfloat16 [16384, 512], P(('blk', 'dp')), may hold values from -10 to 10
- labels: int32 [8192], P(('dp', 'blk')), may hold values from 0 to 16383
Outputs:
- loss: float32 [8192], P(('dp', 'blk'))
All inputs are finite; a program needn't handle non-finite values.
Results may differ from a plain program's by a relative error of at most 0.0017.
Values may be sent and summed in bfloat16 or wider, within the bound.
A program may use at most 128 MiB of HBM per device.

v0:
```python
import math

import jax
import jax.numpy as jnp
from jax import lax
from jax.sharding import PartitionSpec as P

EPSILON = 1e-06
LOGIT_SCALE = 30.0
MARGIN = 0.5


def unit_rows(matrix):
    values = matrix.astype(jnp.float32)
    return (values * lax.rsqrt(jnp.sum(values * values, axis=1, keepdims=True) + EPSILON)).astype(
        jnp.bfloat16
    )


def margin_loss(other_sum, target_cos):
    sine = jnp.sqrt(jnp.maximum(1.0 - target_cos * target_cos, 0.0))
    shifted = target_cos * math.cos(MARGIN) - sine * math.sin(MARGIN)
    return (
        LOGIT_SCALE
        + jnp.log(other_sum + jnp.exp(LOGIT_SCALE * shifted - LOGIT_SCALE))
        - LOGIT_SCALE * shifted
    )


def block_terms(rows, row_labels, centers_block, class_start):
    cosine = jnp.einsum("nd,cd->nc", rows, centers_block, preferred_element_type=jnp.float32)
    columns = class_start + jnp.arange(centers_block.shape[0], dtype=jnp.int32)
    is_target = row_labels[:, None] == columns[None, :]
    other_sum = jnp.sum(
        jnp.where(is_target, 0.0, jnp.exp(LOGIT_SCALE * cosine - LOGIT_SCALE)), axis=1
    )
    target_cos = jnp.sum(jnp.where(is_target, cosine, 0.0), axis=1)
    return (other_sum, target_cos)


def body(embeddings, centers, labels):
    emb_unit = unit_rows(embeddings)
    center_unit = unit_rows(centers)
    shard_classes = center_unit.shape[0]
    group_count = lax.axis_size("dp")
    group_index = lax.axis_index("dp")
    group_rows, group_labels = (
        lax.all_gather(emb_unit, "dp", axis=0, tiled=True),
        lax.all_gather(labels, "dp", axis=0, tiled=True),
    )
    group_total = group_rows.shape[0]
    zeros_sum = jnp.zeros((group_total,), jnp.float32)
    pieces = lax.all_gather(center_unit, "blk", axis=0, tiled=True)
    span_rows = math.gcd(math.gcd(pieces.shape[0], shard_classes), 512)

    def one_span(accum, step_index):
        first = step_index * span_rows
        block_rows = lax.dynamic_slice_in_dim(pieces, step_index * span_rows, span_rows, 0)
        class_start = (
            first // shard_classes * group_count + group_index
        ) * shard_classes + first % shard_classes
        other_part, target_part = block_terms(group_rows, group_labels, block_rows, class_start)
        return ((accum[0] + other_part, accum[1] + target_part), None)

    result, ignored = lax.scan(
        one_span, (zeros_sum, zeros_sum), jnp.arange(pieces.shape[0] // span_rows, dtype=jnp.int32)
    )
    other_group, target_group = result
    other_sum, target_cos = (
        lax.psum_scatter(other_group, "dp", scatter_dimension=0, tiled=True),
        lax.psum_scatter(target_group, "dp", scatter_dimension=0, tiled=True),
    )
    return margin_loss(other_sum, target_cos)


def solution(mesh):
    return jax.shard_map(
        body,
        mesh=mesh,
        in_specs=(P(("dp", "blk"), None), P(("blk", "dp"), None), P(("dp", "blk"))),
        out_specs=P(("dp", "blk")),
        check_vma=False,
    )
```

profile of v0, /device:TPU:0, one launch (start us, length us, event | category | flops | bytes accessed | tf_op | source)
XLA Modules:
  0.0 147.6 jit_solution(2375820200223989825)
XLA Ops:
  6.5 0.0 all-gather.6.cloned.1.call-start
  6.5 1.1 fusion.9
  7.7 1.8 %fusion.10 = bf16[256,512]{1,0:T(8,128)(2,1)} fusion(bf16[256,512]{1,0:T(8,128)(2,1)} %param.5, f32[256]{0:T(256)S(1)} %add_rsqrt_fusion.1), kind=kLoop, calls=%fused_computation.20 | loop fusion | flops 393216 | bytes 525312 | tf_op jit(solution)/shard_map/convert_element_type | solution.py:15
  9.4 0.0 all-gather.6.cloned.1.call-update
  9.5 0.0 all-gather.4.cloned.1.call-start
  9.5 1.2 fusion.7
  10.7 2.0 %fusion.8 = bf16[512,512]{1,0:T(8,128)(2,1)} fusion(bf16[512,512]{1,0:T(8,128)(2,1)} %param.6, f32[512]{0:T(512)S(1)} %add_rsqrt_fusion), kind=kLoop, calls=%fused_computation.16 | loop fusion | flops 786432 | bytes 1050624 | tf_op jit(solution)/shard_map/convert_element_type | solution.py:15
  12.7 0.0 all-gather.4.cloned.1.call-update
  12.8 0.0 copy-done.1
  12.8 0.6 dynamic-slice
  14.1 6.0 %all-gather = s32[4,1,256]{2,1,0:T(1,128)S(1)} all-gather(s32[1,1,256]{2,1,0:T(1,128)S(1)} %bitcast.21), channel_id=1, replica_groups=mesh['blk'=8,'dp'=4] {'dp'}, dimensions={0}, use_global_device_ids=true | all-gather | bytes 5120 | tf_op jit(solution)/shard_map/all_gather | solution.py:49
  20.1 8.9 %all-gather.6.cloned.1.call-done = bf16[1024,512]{1,0:T(8,128)(2,1)} async-done(((bf16[256,512]{1,0:T(8,128)(2,1)}), bf16[1024,512]{1,0:T(8,128)(2,1)}) %all-gather.6.cloned.1.call-update) | async-done | bytes 1048592 | tf_op jit(solution)/shard_map/all_gather | solution.py:48
  29.0 75.0 %all-gather.4.cloned.1.call-done = bf16[4096,512]{1,0:T(8,128)(2,1)} async-done(((bf16[512,512]{1,0:T(8,128)(2,1)}), bf16[4096,512]{1,0:T(8,128)(2,1)}) %all-gather.4.cloned.1.call-update) | async-done | bytes 4194320 | tf_op jit(solution)/shard_map/all_gather | solution.py:53
  104.0 30.3 %while.15 = (s32[]{:T(128)}, f32[1024]{0:T(1024)S(1)}, f32[1024]{0:T(1024)S(1)}, s32[1024]{0:T(1024)S(1)}, s32[8]{0:T(128)S(1)}, /*index=5*/s32[]{:T(128)}, bf16...) while((s32[]{:T(128)}, f32[1024]{0:T(1024)S(1)}, ...), condition=%wide.region_5.6_spmd.clone, body=%wide.region_2.5_spmd.clone.sunk | while | flops 540543488 | bytes 1614283 | solution.py:65
  104.0 0.6 dynamic_slice.22
  105.3 2.4 %fusion.18 = (f32[1024]{0:T(1024)S(1)}, f32[1024]{0:T(1024)S(1)}) fusion(s32[1024]{0:T(1024)S(1)} %get-tuple-element.256, s32[512]{0:T(512)S(1)} %iota_add_fusion.2, bf16[1024,512]{1,0:T(8,128)(2,1)} %get-tuple-element.260, bf16[4096,512]{1,0:T(8,128)(2,1)} %get-tuple-element.259, s32[]{:T(128)S(6)} %select_n.57), kind=kOutput, calls=%fused_computation.3.clone.1 | convolution fusion | flops 540538880 | bytes 1587204 | tf_op jit(solution)/shard_map/while/body/eval_jaxpr/nd,cd->nc/dot_general | solution.py:31
  107.8 0.6 dynamic_slice.22
  109.1 2.4 %fusion.18 = (f32[1024]{0:T(1024)S(1)}, f32[1024]{0:T(1024)S(1)}) fusion(s32[1024]{0:T(1024)S(1)} %get-tuple-element.256, s32[512]{0:T(512)S(1)} %iota_add_fusion.2, bf16[1024,512]{1,0:T(8,128)(2,1)} %get-tuple-element.260, bf16[4096,512]{1,0:T(8,128)(2,1)} %get-tuple-element.259, s32[]{:T(128)S(6)} %select_n.57), kind=kOutput, calls=%fused_computation.3.clone.1 | convolution fusion | flops 540538880 | bytes 1587204 | tf_op jit(solution)/shard_map/while/body/eval_jaxpr/nd,cd->nc/dot_general | solution.py:31
  111.6 0.6 dynamic_slice.22
  112.9 2.4 %fusion.18 = (f32[1024]{0:T(1024)S(1)}, f32[1024]{0:T(1024)S(1)}) fusion(s32[1024]{0:T(1024)S(1)} %get-tuple-element.256, s32[512]{0:T(512)S(1)} %iota_add_fusion.2, bf16[1024,512]{1,0:T(8,128)(2,1)} %get-tuple-element.260, bf16[4096,512]{1,0:T(8,128)(2,1)} %get-tuple-element.259, s32[]{:T(128)S(6)} %select_n.57), kind=kOutput, calls=%fused_computation.3.clone.1 | convolution fusion | flops 540538880 | bytes 1587204 | tf_op jit(solution)/shard_map/while/body/eval_jaxpr/nd,cd->nc/dot_general | solution.py:31
  115.4 0.6 dynamic_slice.22
  116.7 2.4 %fusion.18 = (f32[1024]{0:T(1024)S(1)}, f32[1024]{0:T(1024)S(1)}) fusion(s32[1024]{0:T(1024)S(1)} %get-tuple-element.256, s32[512]{0:T(512)S(1)} %iota_add_fusion.2, bf16[1024,512]{1,0:T(8,128)(2,1)} %get-tuple-element.260, bf16[4096,512]{1,0:T(8,128)(2,1)} %get-tuple-element.259, s32[]{:T(128)S(6)} %select_n.57), kind=kOutput, calls=%fused_computation.3.clone.1 | convolution fusion | flops 540538880 | bytes 1587204 | tf_op jit(solution)/shard_map/while/body/eval_jaxpr/nd,cd->nc/dot_general | solution.py:31
  119.2 0.6 dynamic_slice.22
  120.5 2.4 %fusion.18 = (f32[1024]{0:T(1024)S(1)}, f32[1024]{0:T(1024)S(1)}) fusion(s32[1024]{0:T(1024)S(1)} %get-tuple-element.256, s32[512]{0:T(512)S(1)} %iota_add_fusion.2, bf16[1024,512]{1,0:T(8,128)(2,1)} %get-tuple-element.260, bf16[4096,512]{1,0:T(8,128)(2,1)} %get-tuple-element.259, s32[]{:T(128)S(6)} %select_n.57), kind=kOutput, calls=%fused_computation.3.clone.1 | convolution fusion | flops 540538880 | bytes 1587204 | tf_op jit(solution)/shard_map/while/body/eval_jaxpr/nd,cd->nc/dot_general | solution.py:31
  123.0 0.6 dynamic_slice.22
  124.3 2.4 %fusion.18 = (f32[1024]{0:T(1024)S(1)}, f32[1024]{0:T(1024)S(1)}) fusion(s32[1024]{0:T(1024)S(1)} %get-tuple-element.256, s32[512]{0:T(512)S(1)} %iota_add_fusion.2, bf16[1024,512]{1,0:T(8,128)(2,1)} %get-tuple-element.260, bf16[4096,512]{1,0:T(8,128)(2,1)} %get-tuple-element.259, s32[]{:T(128)S(6)} %select_n.57), kind=kOutput, calls=%fused_computation.3.clone.1 | convolution fusion | flops 540538880 | bytes 1587204 | tf_op jit(solution)/shard_map/while/body/eval_jaxpr/nd,cd->nc/dot_general | solution.py:31
  126.8 0.6 dynamic_slice.22
  128.1 2.4 %fusion.18 = (f32[1024]{0:T(1024)S(1)}, f32[1024]{0:T(1024)S(1)}) fusion(s32[1024]{0:T(1024)S(1)} %get-tuple-element.256, s32[512]{0:T(512)S(1)} %iota_add_fusion.2, bf16[1024,512]{1,0:T(8,128)(2,1)} %get-tuple-element.260, bf16[4096,512]{1,0:T(8,128)(2,1)} %get-tuple-element.259, s32[]{:T(128)S(6)} %select_n.57), kind=kOutput, calls=%fused_computation.3.clone.1 | convolution fusion | flops 540538880 | bytes 1587204 | tf_op jit(solution)/shard_map/while/body/eval_jaxpr/nd,cd->nc/dot_general | solution.py:31
  130.5 0.6 dynamic_slice.22
  131.9 2.4 %fusion.18 = (f32[1024]{0:T(1024)S(1)}, f32[1024]{0:T(1024)S(1)}) fusion(s32[1024]{0:T(1024)S(1)} %get-tuple-element.256, s32[512]{0:T(512)S(1)} %iota_add_fusion.2, bf16[1024,512]{1,0:T(8,128)(2,1)} %get-tuple-element.260, bf16[4096,512]{1,0:T(8,128)(2,1)} %get-tuple-element.259, s32[]{:T(128)S(6)} %select_n.57), kind=kOutput, calls=%fused_computation.3.clone.1 | convolution fusion | flops 540538880 | bytes 1587204 | tf_op jit(solution)/shard_map/while/body/eval_jaxpr/nd,cd->nc/dot_general | solution.py:31
  134.3 5.8 %all-reduce.2 = (f32[1024]{0:T(1024)S(1)}, f32[1024]{0:T(1024)S(1)}) all-reduce(f32[1024]{0:T(1024)S(1)} %get-tuple-element.111, f32[1024]{0:T(1024)S(1)} %get-tuple-element.112), channel_id=2, replica_groups=mesh['blk'=8,'dp'=4] {'dp'}, use_global_device_ids=true, to_apply=%region_6.7.clone | all-reduce | flops 2048 | bytes 16384
  140.1 0.7 fusion.13
  (24 shorter events, 0.1 us)
Async XLA Ops:
  6.5 6.3 %copy-start.1 = (u32[32]{0:T(128)S(1)}, u32[32]{0:T(128)}, u32[]{:S(2)}) copy-start(u32[32]{0:T(128)} %constant.103) | copy-start | bytes 388
  6.5 7.5 %copy-start = (s32[256]{0:T(256)S(1)}, s32[256]{0:T(256)}, u32[]{:S(2)}) copy-start(s32[256]{0:T(256)} %param.7) | copy-start | bytes 3076
  6.5 22.5 %all-gather.6.cloned.1.call-start = ((), (), s32[]{:S(2)}) async-start(), calls=%async_computation.1 | async-start | bytes 1310720 | tf_op jit(solution)/shard_map/all_gather | solution.py:48
  9.5 94.5 %all-gather.4.cloned.1.call-start = ((), (), s32[]{:S(2)}) async-start(), calls=%async_computation | async-start | bytes 4718592 | tf_op jit(solution)/shard_map/all_gather | solution.py:53
Sparse Core Ops, SparseCore 0:
  9.6 19.4 all-gather.5
  31.2 72.7 all-gather.3
where the time goes:
time: 148 us
  waiting for transfers between devices  83.9 us (57%)
  matrix products  19.6 us (13%)
  between operations  14.1 us (10%)
  blocking collectives  11.8 us (8%)
  other arithmetic  6.88 us (5%)
  loops' own time  5.78 us (4%)
  local copies, waits for them, and re-layouts  5.52 us (4%)
    all_gather x1, waiting for transfers between devices, body(): pieces = lax.all_gather(center_unit, 'blk', axis=0, tiled=True)  75 us
    dot_general x8, matrix products, block_terms(): jnp.einsum('nd,cd->nc', rows, centers_block, preferred_element_type=jnp.f...  19.6 us
    all_gather x1, waiting for transfers between devices, body(): lax.all_gather(emb_unit, 'dp', axis=0, tiled=True)  8.92 us
    all_gather x1, blocking collectives, body(): lax.all_gather(labels, 'dp', axis=0, tiled=True)  6.04 us
    another operation x1, loops' own time, body(): lax.scan(one_span, (zeros_sum, zeros_sum), jnp.arange(pieces.shape[0] //...  5.78 us
    unnamed x1, blocking collectives  5.77 us
    dynamic_slice x8, local copies, waits for them, and re-layouts, body(): lax.scan(one_span, (zeros_sum, zeros_sum), jnp.arange(pieces.shape[0] //...  4.9 us
    convert_element_type x2, other arithmetic, unit_rows(): (values * lax.rsqrt(jnp.sum(values * values, axis=1, keepdims=True) + EPS...  3.79 us
  transfers between devices with their start and end apart: 2, of which 2 were waited for; matrix products, arithmetic and copies ran while one was open for 3% of the time, Pallas kernels for 0%

commit v1 on v0

v1 whole, which is shorter than its diff:
```python
import functools
import math

import jax
import jax.numpy as jnp
from jax import lax
from jax.experimental import pallas as pl
from jax.experimental.pallas import tpu as pltpu
from jax.sharding import PartitionSpec as P

EPSILON = 1e-06
LOGIT_SCALE = 30.0
MARGIN = 0.5
MESH = pl.DeviceIdType.MESH


def unit_rows(matrix):
    values = matrix.astype(jnp.float32)
    return (values * lax.rsqrt(jnp.sum(values * values, axis=1, keepdims=True) + EPSILON)).astype(
        jnp.bfloat16
    )


def margin_loss(other_sum, target_cos):
    sine = jnp.sqrt(jnp.maximum(1.0 - target_cos * target_cos, 0.0))
    shifted = target_cos * math.cos(MARGIN) - sine * math.sin(MARGIN)
    return (
        LOGIT_SCALE
        + jnp.log(other_sum + jnp.exp(LOGIT_SCALE * shifted - LOGIT_SCALE))
        - LOGIT_SCALE * shifted
    )


def kernel(
    depth,
    emb_ref,
    cen_ref,
    lab_ref,
    out_ref,
    emb_raw,
    sib_raw,
    cen_raw,
    emb_n,
    cen_n,
    labels,
    acc_o,
    acc_t,
    part,
    parts_in,
    bases,
    local_sem,
    lab_send,
    lab_recv,
    row_recv,
    up_send,
    down_send,
    sib_send,
    sib_recv,
    x_send,
    x_recv,
    y_send,
    y_recv,
    part_send,
    part_recv,
):
    blk, dp = lax.axis_index("blk"), lax.axis_index("dp")
    z, x = blk // 2, blk % 2
    y, core = dp // 2, dp % 2
    rows, width = emb_raw.shape[2:]
    quarter = cen_raw.shape[2]
    group = 2 * depth
    here = 2 * z + core
    center_tiles = cen_raw.shape[0]
    center_rounds = center_tiles - 2
    row_rounds = 2 * (depth - 1)
    rounds = max(center_rounds, row_rounds)

    def device(zz, xx, yy, cc):
        return {"blk": 2 * zz + xx, "dp": 2 * yy + cc}

    def member_at(j):
        return lax.rem(z + j // 2, depth), (core + j) % 2

    def member(j):
        zz, cc = member_at(j)
        return device(zz, x, y, cc)

    x_peer = device(z, 1 - x, y, core)
    y_peer = device(z, x, 1 - y, core)
    sibling = device(z, x, y, 1 - core)
    above = device(jnp.minimum(z + 1, depth - 1), x, y, core)
    below = device(jnp.maximum(z - 1, 0), x, y, core)

    def remote(src, dst, send, recv, to):
        return pltpu.make_async_remote_copy(
            src_ref=src, dst_ref=dst, send_sem=send, recv_sem=recv, device_id=to, device_id_type=MESH
        )

    local = [
        pltpu.make_async_copy(cen_ref, cen_raw.at[pl.ds(0, 2)], local_sem.at[0]),
        pltpu.make_async_copy(emb_ref, emb_raw.at[z], local_sem.at[1]),
        pltpu.make_async_copy(lab_ref, labels.at[z, core], local_sem.at[2]),
    ]
    for copy in local:
        copy.start()

    barrier = pltpu.get_barrier_semaphore()
    for j in range(1, group):
        pl.semaphore_signal(barrier, inc=1, device_id=member(j), device_id_type=MESH)
    for to in (x_peer, y_peer):
        pl.semaphore_signal(barrier, inc=1, device_id=to, device_id_type=MESH)

    def block_start(xx, yy):
        return ((2 * z + xx) * 4 + 2 * yy + core) * (4 * quarter)

    own = block_start(x, y)
    from_x, from_y, from_xy = block_start(1 - x, y), block_start(x, 1 - y), block_start(1 - x, 1 - y)
    starts = [own, own + quarter, own + 2 * quarter, own + 3 * quarter]
    for first, second in zip(range(4), (2, 3, 0, 1)):
        starts += [from_x + first * quarter, from_y + second * quarter]
    for first, second in ((2, 0), (3, 1)):
        starts += [from_xy + first * quarter, from_xy + second * quarter]
    for i, start in enumerate(starts):
        bases[i] = start
    acc_o[...] = jnp.zeros_like(acc_o)
    acc_t[...] = jnp.zeros_like(acc_t)

    for copy in local:
        copy.wait()
    pl.semaphore_wait(barrier, group + 1)

    def row_copy(g, sems, to):
        ref = emb_raw.at[g // 2, g % 2]
        return remote(ref, ref, sems.at[g], row_recv.at[g], to)

    def sib_copy(g):
        return remote(
            emb_raw.at[g // 2, g % 2], sib_raw.at[g // 2, g % 2], sib_send.at[g], sib_recv.at[g], sibling
        )

    def x_copy(t, tile, side):
        return remote(cen_raw.at[tile, side], cen_raw.at[t + 1, 0], x_send.at[t], x_recv.at[t], x_peer)

    def y_copy(t, tile, side):
        return remote(cen_raw.at[tile, side], cen_raw.at[t + 1, 1], y_send.at[t], y_recv.at[t], y_peer)

    def lab_copy(j):
        ref = labels.at[z, core]
        return remote(ref, ref, lab_send.at[j], lab_recv.at[j], member(j))

    up_ok, down_ok = z + 1 < depth, z > 0

    def send_up(g):
        @pl.when(up_ok)
        def _():
            row_copy(g, up_send, above).start()

    def send_down(g):
        @pl.when(down_ok)
        def _():
            row_copy(g, down_send, below).start()

    for j in range(1, group):
        lab_copy(j).start()
    send_up(2 * z + 1)
    send_down(2 * z)
    x_copy(1, 0, 0).start()
    y_copy(1, 1, 0).start()
    sib_copy(2 * z).start()
    sib_copy(2 * z + 1).start()
    send_up(2 * z)
    send_down(2 * z + 1)
    x_copy(2, 0, 1).start()
    y_copy(2, 1, 1).start()
    x_copy(3, 1, 0).start()
    y_copy(3, 0, 0).start()
    x_copy(4, 1, 1).start()
    y_copy(4, 0, 1).start()

    def ready_rows(g):
        emb_n[g, core] = unit_rows(emb_raw[g // 2, g % 2])

    def ready_sib(g):
        emb_n[g, 1 - core] = unit_rows(sib_raw[g // 2, g % 2])

    def ready_center(r):
        for side in range(2):
            cen_n[r, side] = unit_rows(cen_raw[r, side])

    def pair(g, r):
        cosine = lax.dot_general(
            cen_n[r].reshape(2 * quarter, width),
            emb_n[g].reshape(2 * rows, width),
            (((1,), (1,)), ((), ())),
            preferred_element_type=jnp.float32,
        )
        label = jnp.concatenate([labels[g // 2, 0, g % 2], labels[g // 2, 1, g % 2]], axis=1)
        index = lax.broadcasted_iota(jnp.int32, (quarter, 2 * rows), 0)
        others, targets = acc_o[g], acc_t[g]
        for side in range(2):
            cos = cosine[side * quarter : (side + 1) * quarter]
            hit = index == label - bases[2 * r + side]
            power = jnp.where(hit, 0.0, jnp.exp2(cos * (LOGIT_SCALE * math.log2(math.e))))
            others += jnp.sum(power.reshape(-1, 8, 2 * rows), axis=0)
            targets += jnp.sum(jnp.where(hit, cos, 0.0).reshape(-1, 8, 2 * rows), axis=0)
        acc_o[g] = others
        acc_t[g] = targets

    def pairs(g_lo, g_hi, r_lo, r_hi):
        @pl.loop(g_lo, g_hi)
        def _(g):
            @pl.loop(r_lo, r_hi)
            def _(r):
                pair(g, r)

    for h in range(2):
        ready_rows(2 * z + h)
        ready_center(h)
    for h in range(2):
        sib_copy(2 * z + h).wait_recv()
        ready_sib(2 * z + h)
    lab_copy(1).wait_recv()
    pairs(2 * z, 2 * z + 2, 0, 2)
    for j in range(2, group):
        lab_copy(j).wait_recv()

    def one_round(t, ignored):
        low, high = 2 * z - t, 2 * z + 1 + t
        has_low, has_high = low >= 0, high < group

        @pl.when(has_low)
        def _():
            row_copy(low, up_send, above).wait_recv()
            sib_copy(low).start()

            @pl.when(up_ok)
            def _():
                row_copy(low, up_send, above).start()

        @pl.when(has_high)
        def _():
            row_copy(high, down_send, below).wait_recv()
            sib_copy(high).start()

            @pl.when(down_ok)
            def _():
                row_copy(high, down_send, below).start()

        @pl.when(t <= center_rounds)
        def _():
            x_copy(t, 0, 0).wait_recv()
            y_copy(t, 0, 0).wait_recv()

        @pl.when(t <= center_rounds - 4)
        def _():
            x_copy(t + 4, t + 1, 1).start()
            y_copy(t + 4, t + 1, 0).start()

        done = jnp.minimum(t, center_rounds) + 1
        g_lo, g_hi = jnp.maximum(low + 1, 0), jnp.minimum(high, group)

        @pl.when(t <= center_rounds)
        def _():
            ready_center(t + 1)

        @pl.when(has_low)
        def _():
            ready_rows(low)

        @pl.when(has_high)
        def _():
            ready_rows(high)

        pairs(g_lo, g_hi, done, jnp.minimum(t + 1, center_rounds + 1) + jnp.where(t <= center_rounds, 1, 0))

        @pl.when(has_low)
        def _():
            sib_copy(low).wait_recv()
            ready_sib(low)

        @pl.when(has_high)
        def _():
            sib_copy(high).wait_recv()
            ready_sib(high)

        last = jnp.minimum(t, center_rounds) + 2
        pairs(low, jnp.where(has_low, low + 1, low), 0, last)
        pairs(high, jnp.where(has_high, high + 1, high), 0, last)
        return ignored

    lax.fori_loop(1, rounds + 1, one_round, 0)

    for g in range(group):
        for quantity, acc in enumerate((acc_o, acc_t)):
            total = jnp.sum(acc[g], axis=0, keepdims=True)
            for cc in range(2):
                part[2 * (g // 2) + cc, quantity, g % 2] = total[:, cc * rows : (cc + 1) * rows]

    def part_copy(j):
        zz, cc = member_at(j)
        return remote(
            part.at[2 * zz + cc], parts_in.at[j], part_send.at[j], part_recv.at[j], member(j)
        )

    for j in range(1, group):
        part_copy(j).start()
    other_sum, target_cos = part[here, 0], part[here, 1]
    for j in range(1, group):
        part_copy(j).wait_recv()
        other_sum += parts_in[j, 0]
        target_cos += parts_in[j, 1]
    out_ref[...] = margin_loss(other_sum * math.exp(-LOGIT_SCALE), target_cos)

    for j in range(1, group):
        lab_copy(j).wait_send()
        part_copy(j).wait_send()
    for t in range(1, center_rounds + 1):
        x_copy(t, 0, 0).wait_send()
        y_copy(t, 0, 0).wait_send()

    @pl.loop(0, group)
    def _(g):
        sib_copy(g).wait_send()

        @pl.when(up_ok & (g < 2 * z + 2))
        def _():
            row_copy(g, up_send, above).wait_send()

        @pl.when(down_ok & (g >= 2 * z))
        def _():
            row_copy(g, down_send, below).wait_send()


def body(depth, embeddings, centers, labels):
    count, width = embeddings.shape
    classes = centers.shape[0]
    rows, quarter, group, tiles = count // 2, classes // 4, 2 * depth, 8
    any_spec = pl.BlockSpec(memory_space=pl.ANY)
    dma = pltpu.SemaphoreType.DMA
    loss = pl.pallas_call(
        functools.partial(kernel, depth),
        out_shape=jax.ShapeDtypeStruct((2, 1, rows), jnp.float32),
        in_specs=[any_spec] * 3,
        out_specs=pl.BlockSpec(memory_space=pltpu.VMEM),
        scratch_shapes=[
            pltpu.VMEM((depth, 2, rows, width), jnp.bfloat16),
            pltpu.VMEM((depth, 2, rows, width), jnp.bfloat16),
            pltpu.VMEM((tiles, 2, quarter, width), jnp.bfloat16),
            pltpu.VMEM((group, 2, rows, width), jnp.bfloat16),
            pltpu.VMEM((tiles, 2, quarter, width), jnp.bfloat16),
            pltpu.VMEM((depth, 2, 2, 1, rows), jnp.int32),
            pltpu.VMEM((group, 8, 2 * rows), jnp.float32),
            pltpu.VMEM((group, 8, 2 * rows), jnp.float32),
            pltpu.VMEM((group, 2, 2, 1, rows), jnp.float32),
            pltpu.VMEM((group, 2, 2, 1, rows), jnp.float32),
            pltpu.SMEM((2 * tiles,), jnp.int32),
            dma((3,)),
            dma((group,)),
            dma((group,)),
            dma((group,)),
            dma((group,)),
            dma((group,)),
            dma((group,)),
            dma((group,)),
            dma((tiles,)),
            dma((tiles,)),
            dma((tiles,)),
            dma((tiles,)),
            dma((group,)),
            dma((group,)),
        ],
        compiler_params=pltpu.CompilerParams(
            collective_id=0, has_side_effects=True, vmem_limit_bytes=48 * 1024 * 1024
        ),
    )(
        embeddings.reshape(2, rows, width),
        centers.reshape(2, 2, quarter, width),
        labels.reshape(2, 1, rows),
    )
    return loss.reshape(-1)


def solution(mesh):
    return jax.shard_map(
        functools.partial(body, mesh.shape["blk"] // 2),
        mesh=mesh,
        in_specs=(P(("dp", "blk"), None), P(("blk", "dp"), None), P(("dp", "blk"))),
        out_specs=P(("dp", "blk")),
        check_vma=False,
    )
```

time: 148 us -> 39.6 us (0.27)
  waiting for transfers between devices: 83.9 us -> 0 us
  Pallas kernels: 0 us -> 36.2 us
  matrix products: 19.6 us -> 0 us
  between operations: 14.1 us -> 0.01 us
  blocking collectives: 11.8 us -> 0 us
  other arithmetic: 6.88 us -> 0 us
  loops' own time: 5.78 us -> 0 us
  local copies, waits for them, and re-layouts: 5.52 us -> 3.23 us
    all_gather x2 -> x0, waiting for transfers between devices: 83.9 us -> none  [the longest x1 75 us: body(): pieces = lax.all_gather(center_unit, 'blk', axis=0, tiled=True)]
    pallas_call x0 -> x1, Pallas kernels: none -> 36.2 us  [body(): pl.pallas_call(functools.partial(kernel, depth), out_shape=jax.ShapeDtype...]
    dot_general x8 -> x0, matrix products: 19.6 us -> none  [block_terms(): jnp.einsum('nd,cd->nc', rows, centers_block, preferred_element_type=jnp.f...]
    all_gather x1 -> x0, blocking collectives: 6.04 us -> none  [body(): lax.all_gather(labels, 'dp', axis=0, tiled=True)]
    another operation x1 -> x0, loops' own time: 5.78 us -> none  [body(): lax.scan(one_span, (zeros_sum, zeros_sum), jnp.arange(pieces.shape[0] //...]
    unnamed x1 -> x0, blocking collectives: 5.77 us -> none
    dynamic_slice x8 -> x0, local copies, waits for them, and re-layouts: 4.9 us -> none  [body(): lax.scan(one_span, (zeros_sum, zeros_sum), jnp.arange(pieces.shape[0] //...]
    convert_element_type x2 -> x0, other arithmetic: 3.79 us -> none  [unit_rows(): (values * lax.rsqrt(jnp.sum(values * values, axis=1, keepdims=True) + EPS...]
  transfers between devices with their start and end apart: 2 -> 0, of which waited for: 2 -> 0; matrix products, arithmetic and copies ran while one was open for 3% -> 0% of each run, Pallas kernels for 0% -> 0%
where the time goes in v1:
time: 39.6 us; the launch traced here: 39.4 us
  Pallas kernels  36.2 us (91%)
  local copies, waits for them, and re-layouts  3.23 us (8%)
    pallas_call x1, Pallas kernels, body(): pl.pallas_call(functools.partial(kernel, depth), out_shape=jax.ShapeDtype...  36.2 us
    unnamed x7, local copies, waits for them, and re-layouts  3.23 us

profile of v1, /device:TPU:0, one launch (start us, length us, event | category | flops | bytes accessed | tf_op | source)
XLA Modules:
  0.0 39.4 jit_solution(11067213849930539392)
XLA Ops:
  0.0 0.0 copy-start.2
  0.0 0.7 %copy-done.2 = s32[256]{0:T(256)S(1)} copy-done((s32[256]{0:T(256)S(1)}, s32[256]{0:T(256)}, u32[]{:S(2)}) %copy-start.2) | copy-done | bytes 1048
  0.7 0.0 copy-start
  0.7 1.0 %copy-done = bf16[512,512]{1,0:T(8,128)(2,1)S(1)} copy-done((bf16[512,512]{1,0:T(8,128)(2,1)S(1)}, bf16[512,512]{1,0:T(8,128)(2,1)}, u32[]{:S(2)}) %copy-start) | copy-done | bytes 524312
  1.7 0.0 copy-start.1
  1.7 0.9 %copy-done.1 = bf16[256,512]{1,0:T(8,128)(2,1)S(1)} copy-done((bf16[256,512]{1,0:T(8,128)(2,1)S(1)}, bf16[256,512]{1,0:T(8,128)(2,1)}, u32[]{:S(2)}) %copy-start.1) | copy-done | bytes 262168
  2.7 36.2 %shard_map.37 = f32[2,1,128]{2,1,0:T(1,128)S(1)} custom-call(bf16[2,128,512]{2,1,0:T(8,128)(2,1)S(1)} %bitcast.5, bf16[2,2,128,512]{3,2,1,0:T(8,128)(2,1)S(1)} %bitcast.4, s32[2,1,128]{2,1,0:T(1,128)S(1)} %bitcast.7), custom_call_target="tpu_custom_call" | custom-call | tf_op jit(solution)/shard_map/pallas_call | solution.py:340
  38.9 0.6 %copy.5 = f32[256]{0:T(256)} copy(f32[256]{0:T(256)S(1)} %bitcast.6) | data formatting | bytes 2048
Async XLA Ops:
  0.0 0.7 %copy-start.2 = (s32[256]{0:T(256)S(1)}, s32[256]{0:T(256)}, u32[]{:S(2)}) copy-start(s32[256]{0:T(256)} %param.5) | copy-start | bytes 3076
  0.7 1.0 %copy-start = (bf16[512,512]{1,0:T(8,128)(2,1)S(1)}, bf16[512,512]{1,0:T(8,128)(2,1)}, u32[]{:S(2)}) copy-start(bf16[512,512]{1,0:T(8,128)(2,1)} %param.4) | copy-start | bytes 1572868
  1.7 0.9 %copy-start.1 = (bf16[256,512]{1,0:T(8,128)(2,1)S(1)}, bf16[256,512]{1,0:T(8,128)(2,1)}, u32[]{:S(2)}) copy-start(bf16[256,512]{1,0:T(8,128)(2,1)} %param.3) | copy-start | bytes 786436

commit v2 on v1

--- a/solution.py
+++ b/solution.py
@@ -51,11 +51,8 @@
     local_sem,
     lab_send,
     lab_recv,
+    row_send,
     row_recv,
-    up_send,
-    down_send,
-    sib_send,
-    sib_recv,
     x_send,
     x_recv,
     y_send,
@@ -104,11 +101,18 @@
     for copy in local:
         copy.start()
 
+    up_ok, down_ok = z + 1 < depth, z > 0
     barrier = pltpu.get_barrier_semaphore()
-    for j in range(1, group):
-        pl.semaphore_signal(barrier, inc=1, device_id=member(j), device_id_type=MESH)
-    for to in (x_peer, y_peer):
+    for to in (sibling, x_peer, y_peer):
         pl.semaphore_signal(barrier, inc=1, device_id=to, device_id_type=MESH)
+
+    @pl.when(up_ok)
+    def _():
+        pl.semaphore_signal(barrier, inc=1, device_id=above, device_id_type=MESH)
+
+    @pl.when(down_ok)
+    def _():
+        pl.semaphore_signal(barrier, inc=1, device_id=below, device_id_type=MESH)
 
     def block_start(xx, yy):
         return ((2 * z + xx) * 4 + 2 * yy + core) * (4 * quarter)
@@ -127,16 +131,49 @@
 
     for copy in local:
         copy.wait()
-    pl.semaphore_wait(barrier, group + 1)
-
-    def row_copy(g, sems, to):
-        ref = emb_raw.at[g // 2, g % 2]
-        return remote(ref, ref, sems.at[g], row_recv.at[g], to)
+    pl.semaphore_wait(barrier, 3 + jnp.where(up_ok, 1, 0) + jnp.where(down_ok, 1, 0))
+
+    class Pair:
+        def __init__(self, *copies):
+            self.copies = copies
+
+        def start(self):
+            for copy in self.copies:
+                copy.start()
+
+        def wait_recv(self):
+            for copy in self.copies:
+                copy.wait_recv()
+
+        def wait_send(self):
+            for copy in self.copies:
+                copy.wait_send()
+
+    def row_copy(g, way, to):
+        ref, tags = emb_raw.at[g // 2, g % 2], labels.at[g // 2, core, g % 2]
+        return Pair(
+            remote(tags, tags, lab_send.at[way, g], lab_recv.at[0, g], to),
+            remote(ref, ref, row_send.at[way, g], row_recv.at[0, g], to),
+        )
 
     def sib_copy(g):
-        return remote(
-            emb_raw.at[g // 2, g % 2], sib_raw.at[g // 2, g % 2], sib_send.at[g], sib_recv.at[g], sibling
+        tags = labels.at[g // 2, core, g % 2]
+        return Pair(
+            remote(tags, tags, lab_send.at[2, g], lab_recv.at[1, g], sibling),
+            remote(
+                emb_raw.at[g // 2, g % 2],
+                sib_raw.at[g // 2, g % 2],
+                row_send.at[2, g],
+                row_recv.at[1, g],
+                sibling,
+            ),
         )
+
+    def up_copy(g):
+        return row_copy(g, 0, above)
+
+    def down_copy(g):
+        return row_copy(g, 1, below)
 
     def x_copy(t, tile, side):
         return remote(cen_raw.at[tile, side], cen_raw.at[t + 1, 0], x_send.at[t], x_recv.at[t], x_peer)
@@ -144,24 +181,18 @@
     def y_copy(t, tile, side):
         return remote(cen_raw.at[tile, side], cen_raw.at[t + 1, 1], y_send.at[t], y_recv.at[t], y_peer)
 
-    def lab_copy(j):
-        ref = labels.at[z, core]
-        return remote(ref, ref, lab_send.at[j], lab_recv.at[j], member(j))
-
-    up_ok, down_ok = z + 1 < depth, z > 0
+    def part_copy(j):
+        zz, cc = member_at(j)
+        return remote(
+            part.at[2 * zz + cc], parts_in.at[j], part_send.at[j], part_recv.at[j], member(j)
+        )
 
     def send_up(g):
-        @pl.when(up_ok)
-        def _():
-            row_copy(g, up_send, above).start()
+        pl.when(up_ok)(lambda: up_copy(g).start())
 
     def send_down(g):
-        @pl.when(down_ok)
-        def _():
-            row_copy(g, down_send, below).start()
-
-    for j in range(1, group):
-        lab_copy(j).start()
+        pl.when(down_ok)(lambda: down_copy(g).start())
+
     send_up(2 * z + 1)
     send_down(2 * z)
     x_copy(1, 0, 0).start()
@@ -187,31 +218,33 @@
         for side in range(2):
             cen_n[r, side] = unit_rows(cen_raw[r, side])
 
-    def pair(g, r):
+    def add_terms(g, first, last, others, targets):
         cosine = lax.dot_general(
-            cen_n[r].reshape(2 * quarter, width),
+            cen_n[first:last].reshape(-1, width),
             emb_n[g].reshape(2 * rows, width),
             (((1,), (1,)), ((), ())),
             preferred_element_type=jnp.float32,
         )
         label = jnp.concatenate([labels[g // 2, 0, g % 2], labels[g // 2, 1, g % 2]], axis=1)
-        index = lax.broadcasted_iota(jnp.int32, (quarter, 2 * rows), 0)
-        others, targets = acc_o[g], acc_t[g]
-        for side in range(2):
-            cos = cosine[side * quarter : (side + 1) * quarter]
-            hit = index == label - bases[2 * r + side]
-            power = jnp.where(hit, 0.0, jnp.exp2(cos * (LOGIT_SCALE * math.log2(math.e))))
-            others += jnp.sum(power.reshape(-1, 8, 2 * rows), axis=0)
-            targets += jnp.sum(jnp.where(hit, cos, 0.0).reshape(-1, 8, 2 * rows), axis=0)
-        acc_o[g] = others
-        acc_t[g] = targets
-
-    def pairs(g_lo, g_hi, r_lo, r_hi):
-        @pl.loop(g_lo, g_hi)
-        def _(g):
-            @pl.loop(r_lo, r_hi)
-            def _(r):
-                pair(g, r)
+        label = label - lax.broadcasted_iota(jnp.int32, (8, 2 * rows), 0)
+        for m in range(2 * (last - first)):
+            local = label - bases[2 * first + m]
+            for q in range(0, quarter, 8):
+                cos = cosine[m * quarter + q : m * quarter + q + 8]
+                hit = local == q
+                power = jnp.exp2(cos * (LOGIT_SCALE * math.log2(math.e)))
+                others = others + jnp.where(hit, 0.0, power)
+                targets = jnp.where(hit, cos, targets)
+        return others, targets
+
+    def pair(g, first, last):
+        acc_o[g], acc_t[g] = add_terms(g, first, last, acc_o[g], acc_t[g])
+
+    def blocks(lo, hi, first, last):
+        @pl.loop(lo, hi)
+        def _(zz):
+            pair(2 * zz, first, last)
+            pair(2 * zz + 1, first, last)
 
     for h in range(2):
         ready_rows(2 * z + h)
@@ -219,91 +252,94 @@
     for h in range(2):
         sib_copy(2 * z + h).wait_recv()
         ready_sib(2 * z + h)
-    lab_copy(1).wait_recv()
-    pairs(2 * z, 2 * z + 2, 0, 2)
-    for j in range(2, group):
-        lab_copy(j).wait_recv()
-
-    def one_round(t, ignored):
+    blocks(z, z + 1, 0, 2)
+
+    def receive_rows(t):
         low, high = 2 * z - t, 2 * z + 1 + t
         has_low, has_high = low >= 0, high < group
 
         @pl.when(has_low)
         def _():
-            row_copy(low, up_send, above).wait_recv()
+            up_copy(low).wait_recv()
             sib_copy(low).start()
-
-            @pl.when(up_ok)
-            def _():
-                row_copy(low, up_send, above).start()
+            send_up(low)
 
         @pl.when(has_high)
         def _():
-            row_copy(high, down_send, below).wait_recv()
+            down_copy(high).wait_recv()
             sib_copy(high).start()
-
-            @pl.when(down_ok)
-            def _():
-                row_copy(high, down_send, below).start()
-
-        @pl.when(t <= center_rounds)
-        def _():
-            x_copy(t, 0, 0).wait_recv()
-            y_copy(t, 0, 0).wait_recv()
-
-        @pl.when(t <= center_rounds - 4)
-        def _():
+            send_down(high)
+
+    def receive_centers(t):
+        x_copy(t, 0, 0).wait_recv()
+        y_copy(t, 0, 0).wait_recv()
+        if t <= center_rounds - 4:
             x_copy(t + 4, t + 1, 1).start()
             y_copy(t + 4, t + 1, 0).start()
 
-        done = jnp.minimum(t, center_rounds) + 1
-        g_lo, g_hi = jnp.maximum(low + 1, 0), jnp.minimum(high, group)
-
-        @pl.when(t <= center_rounds)
+    def use_rows(t, tiles):
+        low, high = 2 * z - t, 2 * z + 1 + t
+        count = jnp.where(low >= 0, 1, 0) + jnp.where(high < group, 1, 0)
+
+        @pl.loop(0, count)
+        def _(i):
+            g = jnp.where((low >= 0) & (i == 0), low, high)
+            ready_rows(g)
+            sib_copy(g).wait_recv()
+            ready_sib(g)
+            pair(g, 0, tiles)
+
+    def span(t):
+        return jnp.maximum(z - t // 2, 0), jnp.minimum(z + 1 + t // 2, depth)
+
+    tiles = 2
+    for t in range(1, min(rounds, center_rounds + 1)):
+        receive_rows(t)
+        receive_centers(t)
+        ready_center(t + 1)
+        if t == center_rounds - 1:
+            blocks(*span(t - 1), tiles, t + 2)
+            tiles = t + 2
+        use_rows(t, tiles)
+        if t % 2 == 0 and t < center_rounds:
+            blocks(*span(t), tiles, t + 2)
+            tiles = t + 2
+    if rounds > center_rounds:
+
+        @pl.loop(center_rounds + 1, rounds)
+        def _(t):
+            receive_rows(t)
+            use_rows(t, tiles)
+
+    receive_rows(rounds)
+    if rounds == center_rounds:
+        receive_centers(rounds)
+        ready_center(rounds + 1)
+
+    @pl.loop(0, depth)
+    def _(i):
+        zz = jnp.where(2 * z < depth, i, depth - 1 - i)
+
+        @pl.when(i == depth - 1)
         def _():
-            ready_center(t + 1)
-
-        @pl.when(has_low)
+            use_rows(rounds, tiles)
+
+        for h in range(2):
+            g = 2 * zz + h
+            sums = add_terms(g, tiles, center_tiles, acc_o[g], acc_t[g])
+            for quantity, total in enumerate(sums):
+                total = jnp.sum(total, axis=0, keepdims=True)
+                for cc in range(2):
+                    part[2 * zz + cc, quantity, h] = total[:, cc * rows : (cc + 1) * rows]
+
+        step = lax.rem(zz + depth - z, depth)
+
+        @pl.when(step > 0)
         def _():
-            ready_rows(low)
-
-        @pl.when(has_high)
-        def _():
-            ready_rows(high)
-
-        pairs(g_lo, g_hi, done, jnp.minimum(t + 1, center_rounds + 1) + jnp.where(t <= center_rounds, 1, 0))
-
-        @pl.when(has_low)
-        def _():
-            sib_copy(low).wait_recv()
-            ready_sib(low)
-
-        @pl.when(has_high)
-        def _():
-            sib_copy(high).wait_recv()
-            ready_sib(high)
-
-        last = jnp.minimum(t, center_rounds) + 2
-        pairs(low, jnp.where(has_low, low + 1, low), 0, last)
-        pairs(high, jnp.where(has_high, high + 1, high), 0, last)
-        return ignored
-
-    lax.fori_loop(1, rounds + 1, one_round, 0)
-
-    for g in range(group):
-        for quantity, acc in enumerate((acc_o, acc_t)):
-            total = jnp.sum(acc[g], axis=0, keepdims=True)
-            for cc in range(2):
-                part[2 * (g // 2) + cc, quantity, g % 2] = total[:, cc * rows : (cc + 1) * rows]
-
-    def part_copy(j):
-        zz, cc = member_at(j)
-        return remote(
-            part.at[2 * zz + cc], parts_in.at[j], part_send.at[j], part_recv.at[j], member(j)
-        )
-
-    for j in range(1, group):
-        part_copy(j).start()
+            part_copy(2 * step).start()
+
+        part_copy(2 * step + 1).start()
+
     other_sum, target_cos = part[here, 0], part[here, 1]
     for j in range(1, group):
         part_copy(j).wait_recv()
@@ -312,7 +348,6 @@
     out_ref[...] = margin_loss(other_sum * math.exp(-LOGIT_SCALE), target_cos)
 
     for j in range(1, group):
-        lab_copy(j).wait_send()
         part_copy(j).wait_send()
     for t in range(1, center_rounds + 1):
         x_copy(t, 0, 0).wait_send()
@@ -321,14 +356,8 @@
     @pl.loop(0, group)
     def _(g):
         sib_copy(g).wait_send()
-
-        @pl.when(up_ok & (g < 2 * z + 2))
-        def _():
-            row_copy(g, up_send, above).wait_send()
-
-        @pl.when(down_ok & (g >= 2 * z))
-        def _():
-            row_copy(g, down_send, below).wait_send()
+        pl.when(up_ok & (g < 2 * z + 2))(lambda: up_copy(g).wait_send())
+        pl.when(down_ok & (g >= 2 * z))(lambda: down_copy(g).wait_send())
 
 
 def body(depth, embeddings, centers, labels):
@@ -355,13 +384,10 @@
             pltpu.VMEM((group, 2, 2, 1, rows), jnp.float32),
             pltpu.SMEM((2 * tiles,), jnp.int32),
             dma((3,)),
-            dma((group,)),
-            dma((group,)),
-            dma((group,)),
-            dma((group,)),
-            dma((group,)),
-            dma((group,)),
-            dma((group,)),
+            dma((3, group)),
+            dma((2, group)),
+            dma((3, group)),
+            dma((2, group)),
             dma((tiles,)),
             dma((tiles,)),
             dma((tiles,)),

time: 39.6 us -> 35 us (0.88)
  Pallas kernels: 36.2 us -> 31.6 us
    pallas_call x1, Pallas kernels: 36.2 us -> 31.6 us  [body(): pl.pallas_call(functools.partial(kernel, depth), out_shape=jax.ShapeDtype...]
where the time goes in v2:
time: 35 us; the launch traced here: 34.8 us
  Pallas kernels  31.6 us (90%)
  local copies, waits for them, and re-layouts  3.23 us (9%)
    pallas_call x1, Pallas kernels, body(): pl.pallas_call(functools.partial(kernel, depth), out_shape=jax.ShapeDtype...  31.6 us
    unnamed x7, local copies, waits for them, and re-layouts  3.23 us

profile of v2, /device:TPU:0, one launch (start us, length us, event | category | flops | bytes accessed | tf_op | source)
XLA Modules:
  0.0 34.8 jit_solution(10294023481868319022)
XLA Ops:
  0.0 0.0 copy-start.2
  0.0 0.7 %copy-done.2 = s32[256]{0:T(256)S(1)} copy-done((s32[256]{0:T(256)S(1)}, s32[256]{0:T(256)}, u32[]{:S(2)}) %copy-start.2) | copy-done | bytes 1048
  0.7 0.0 copy-start
  0.7 1.0 %copy-done = bf16[512,512]{1,0:T(8,128)(2,1)S(1)} copy-done((bf16[512,512]{1,0:T(8,128)(2,1)S(1)}, bf16[512,512]{1,0:T(8,128)(2,1)}, u32[]{:S(2)}) %copy-start) | copy-done | bytes 524312
  1.7 0.0 copy-start.1
  1.7 0.9 %copy-done.1 = bf16[256,512]{1,0:T(8,128)(2,1)S(1)} copy-done((bf16[256,512]{1,0:T(8,128)(2,1)S(1)}, bf16[256,512]{1,0:T(8,128)(2,1)}, u32[]{:S(2)}) %copy-start.1) | copy-done | bytes 262168
  2.7 31.6 %shard_map.37 = f32[2,1,128]{2,1,0:T(1,128)S(1)} custom-call(bf16[2,128,512]{2,1,0:T(8,128)(2,1)S(1)} %bitcast.5, bf16[2,2,128,512]{3,2,1,0:T(8,128)(2,1)S(1)} %bitcast.4, s32[2,1,128]{2,1,0:T(1,128)S(1)} %bitcast.7), custom_call_target="tpu_custom_call" | custom-call | tf_op jit(solution)/shard_map/pallas_call | solution.py:369
  34.3 0.6 %copy.5 = f32[256]{0:T(256)} copy(f32[256]{0:T(256)S(1)} %bitcast.6) | data formatting | bytes 2048
Async XLA Ops:
  0.0 0.7 %copy-start.2 = (s32[256]{0:T(256)S(1)}, s32[256]{0:T(256)}, u32[]{:S(2)}) copy-start(s32[256]{0:T(256)} %param.5) | copy-start | bytes 3076
  0.7 1.0 %copy-start = (bf16[512,512]{1,0:T(8,128)(2,1)S(1)}, bf16[512,512]{1,0:T(8,128)(2,1)}, u32[]{:S(2)}) copy-start(bf16[512,512]{1,0:T(8,128)(2,1)} %param.4) | copy-start | bytes 1572868
  1.7 0.9 %copy-start.1 = (bf16[256,512]{1,0:T(8,128)(2,1)S(1)}, bf16[256,512]{1,0:T(8,128)(2,1)}, u32[]{:S(2)}) copy-start(bf16[256,512]{1,0:T(8,128)(2,1)} %param.3) | copy-start | bytes 786436

commit v3 on v2

--- a/solution.py
+++ b/solution.py
@@ -316,29 +316,45 @@
         receive_centers(rounds)
         ready_center(rounds + 1)
 
-    @pl.loop(0, depth)
-    def _(i):
-        zz = jnp.where(2 * z < depth, i, depth - 1 - i)
-
-        @pl.when(i == depth - 1)
-        def _():
-            use_rows(rounds, tiles)
-
-        for h in range(2):
-            g = 2 * zz + h
-            sums = add_terms(g, tiles, center_tiles, acc_o[g], acc_t[g])
-            for quantity, total in enumerate(sums):
-                total = jnp.sum(total, axis=0, keepdims=True)
-                for cc in range(2):
-                    part[2 * zz + cc, quantity, h] = total[:, cc * rows : (cc + 1) * rows]
-
+    low_half = 2 * z < depth
+
+    def give(g, sums):
+        for quantity, total in enumerate(sums):
+            total = jnp.sum(total, axis=0, keepdims=True)
+            for cc in range(2):
+                part[2 * (g // 2) + cc, quantity, g % 2] = total[:, cc * rows : (cc + 1) * rows]
+
+    def send_parts(zz):
         step = lax.rem(zz + depth - z, depth)
-
-        @pl.when(step > 0)
-        def _():
-            part_copy(2 * step).start()
-
+        pl.when(step > 0)(lambda: part_copy(2 * step).start())
         part_copy(2 * step + 1).start()
+
+    def place(j):
+        return jnp.where(low_half, j, group - 1 - j)
+
+    early = [place(j) for j in range(group - 1)]
+    for first in range(0, group - 1, 7):
+        some = early[first : first + 7]
+        sums = [add_terms(g, tiles, center_tiles, acc_o[g], acc_t[g]) for g in some]
+        for g, pair_sums in zip(some, sums):
+            give(g, pair_sums)
+    for i in range(depth - 1):
+        send_parts(place(2 * i) // 2)
+
+    final = place(group - 1)
+
+    @pl.when(up_ok & down_ok)
+    def _():
+        give(final, add_terms(final, tiles, center_tiles, acc_o[final], acc_t[final]))
+
+    @pl.when(jnp.logical_not(up_ok & down_ok))
+    def _():
+        ready_rows(final)
+        sib_copy(final).wait_recv()
+        ready_sib(final)
+        give(final, add_terms(final, 0, center_tiles, acc_o[final], acc_t[final]))
+
+    send_parts(final // 2)
 
     other_sum, target_cos = part[here, 0], part[here, 1]
     for j in range(1, group):
@@ -364,7 +380,7 @@
     count, width = embeddings.shape
     classes = centers.shape[0]
     rows, quarter, group, tiles = count // 2, classes // 4, 2 * depth, 8
-    any_spec = pl.BlockSpec(memory_space=pl.ANY)
+    any_spec = pl.BlockSpec(memory_space=pltpu.HBM)
     dma = pltpu.SemaphoreType.DMA
     loss = pl.pallas_call(
         functools.partial(kernel, depth),
@@ -396,7 +412,7 @@
             dma((group,)),
         ],
         compiler_params=pltpu.CompilerParams(
-            collective_id=0, has_side_effects=True, vmem_limit_bytes=48 * 1024 * 1024
+            collective_id=0, has_side_effects=True, vmem_limit_bytes=60 * 1024 * 1024
         ),
     )(
         embeddings.reshape(2, rows, width),

time: 35 us -> 32.7 us (0.934)
  local copies, waits for them, and re-layouts: 3.23 us -> 1.22 us
    unnamed x7 -> x3, local copies, waits for them, and re-layouts: 3.23 us -> 1.22 us
where the time goes in v3:
time: 32.7 us; the launch traced here: 32.5 us
  Pallas kernels  31.3 us (96%)
  local copies, waits for them, and re-layouts  1.22 us (4%)
    pallas_call x1, Pallas kernels, body(): pl.pallas_call(functools.partial(kernel, depth), out_shape=jax.ShapeDtype...  31.3 us
    unnamed x3, local copies, waits for them, and re-layouts  1.22 us

profile of v3, /device:TPU:0, one launch (start us, length us, event | category | flops | bytes accessed | tf_op | source)
XLA Modules:
  0.0 32.5 jit_solution(16440517669278032582)
XLA Ops:
  0.0 31.3 %shard_map.37 = f32[2,1,128]{2,1,0:T(1,128)} custom-call(bf16[2,128,512]{2,1,0:T(8,128)(2,1)} %bitcast.5, bf16[2,2,128,512]{3,2,1,0:T(8,128)(2,1)} %bitcast.4, s32[2,1,128]{2,1,0:T(1,128)} %bitcast.7), custom_call_target="tpu_custom_call" | custom-call | tf_op jit(solution)/shard_map/pallas_call | solution.py:385
  31.3 0.0 copy-start
  31.3 0.7 %copy-done = f32[2,1,128]{2,1,0:T(1,128)S(1)} copy-done((f32[2,1,128]{2,1,0:T(1,128)S(1)}, f32[2,1,128]{2,1,0:T(1,128)}, u32[]{:S(2)}) %copy-start) | copy-done | bytes 1048
  32.0 0.6 %copy.5 = f32[256]{0:T(256)} copy(f32[256]{0:T(256)S(1)} %bitcast.6) | data formatting | bytes 2048
Async XLA Ops:
  31.3 0.7 %copy-start = (f32[2,1,128]{2,1,0:T(1,128)S(1)}, f32[2,1,128]{2,1,0:T(1,128)}, u32[]{:S(2)}) copy-start(f32[2,1,128]{2,1,0:T(1,128)} %shard_map.37) | copy-start | bytes 3076
